TPU v7x, 32 devices: a 4x4x1 block of a 4x4x8 slice. The times are simulated.
32 devices in a mesh: dp: 2 (over z, core), tp: 16 (over x, y).
Axes of the slice: x: 4, y: 4, z: 1, core: 2. Of those that a mesh axis runs over, the one named last changes fastest.
The devices are a block of a 4x4x8 slice.
Arguments:
- x: bfloat16 [5120, 7168], P(('dp', 'tp')), parts along dimension 0
- dy: bfloat16 [5120, 7168], P(('dp', 'tp')), parts along dimension 0
- pre: bfloat16 [5120, 28672], P('dp', 'tp'), parts along dimension 0
- w_in: bfloat16 [7168, 28672], P(None, 'tp')
- w_down: bfloat16 [28672, 7168], P('tp')
Outputs:
- output 1: bfloat16 [5120, 7168], P(('dp', 'tp')), parts along dimension 0
- output 2: bfloat16 [14336, 28672], P('dp', 'tp'), parts along dimension 0
- output 3: bfloat16 [57344, 7168], P(('dp', 'tp')), parts along dimension 0
There are 2 independent parts. A program takes and returns all parts, laid end to end along the dimension named above; an argument that names none is the same for every part.
All inputs are finite; a program needn't handle non-finite values.
Results may differ from a plain program's by a relative error of at most 0.012.
Values are sent between devices in bfloat16 or wider.
A program may use at most 768 MiB of HBM per device.

v0:
```python
import jax
import jax.numpy as jnp


def act(pre):
    return jax.nn.gelu(pre)


def solution(mesh):
    def step(x, dy, pre, w_in, w_down):
        hidden, back = jax.vjp(act, pre.astype(jnp.float32))
        d_hidden = jnp.dot(dy, w_down.T, preferred_element_type=jnp.float32)
        d_pre = back(d_hidden)[0].astype(jnp.bfloat16)
        dx = jnp.dot(d_pre, w_in.T)
        groups = mesh.shape["dp"]

        def by_group(a, b):
            a, b = (t.reshape(groups, -1, t.shape[-1]) for t in (a, b))
            product = jnp.einsum("gta,gtb->gab", a, b, preferred_element_type=jnp.float32)
            return product.astype(jnp.bfloat16).reshape(-1, b.shape[-1])

        return dx, by_group(x, d_pre), by_group(hidden.astype(jnp.bfloat16), dy)

    return step
```

profile of v0, /device:TPU:97, one launch (start us, length us, event | category | flops | bytes accessed | tf_op | source)
XLA Modules:
  0.0 694.5 jit_solution(10950946144157290520)
XLA Ops:
  7.2 0.1 all-gather.10.cloned.1.call-start
  7.2 0.7 all-gather.10.cloned.1.call-update
  8.0 0.1 all-gather.12.cloned.1.call-start
  8.0 0.7 all-gather.12.cloned.1.call-update
  8.8 0.1 reduce-scatter.4.cloned.1.call-start
  8.9 212.8 %all-gather.10.cloned.1.call-done = bf16[2560,7168]{1,0:T(8,128)(2,1)} async-done(((bf16[160,7168]{1,0:T(8,128)(2,1)}), bf16[2560,7168]{1,0:T(8,128)(2,1)}) %all-gather.10.cloned.1.call-update) | async-done | bytes 36700176 | tf_op args[1]
  221.6 76.2 %fusion.23 = f32[2560,1792]{1,0:T(8,128)} fusion(bf16[2560,7168]{1,0:T(8,128)(2,1)} %all-gather.10.cloned.1.call-done, bf16[1792,7168]{1,0:T(8,128)(2,1)} %param.1), kind=kOutput, calls=%fused_computation.27 | convolution fusion | flops 65766686720 | bytes 80740352 | tf_op jit(solution)/dot_general | solution.py:12
  297.9 106.1 %fusion.20 = bf16[2560,7168]{1,0:T(8,128)(2,1)} fusion(bf16[7168,1792]{1,0:T(8,128)(2,1)} %param.3, bf16[2560,1792]{1,0:T(8,128)(2,1)} %param.2, f32[2560,1792]{1,0:T(8,128)} %fusion.23), kind=kOutput, calls=%fused_computation.26 | convolution fusion | flops 65863024640 | bytes 89915392 | tf_op jit(solution)/dot_general | solution.py:14
  403.9 0.1 reduce-scatter.4.cloned.1.call-update
  404.0 27.2 %all-gather.12.cloned.1.call-done = bf16[2560,7168]{1,0:T(8,128)(2,1)} async-done(((bf16[160,7168]{1,0:T(8,128)(2,1)}), bf16[2560,7168]{1,0:T(8,128)(2,1)}) %all-gather.12.cloned.1.call-update) | async-done | bytes 36700176 | tf_op jit(solution)/reshape | solution.py:18
  431.2 117.4 %fusion.1 = bf16[7168,1792]{0,1:T(8,128)(2,1)} fusion(bf16[2560,7168]{1,0:T(8,128)(2,1)} %all-gather.12.cloned.1.call-done, bf16[2560,1792]{1,0:T(8,128)(2,1)} %param.2, f32[2560,1792]{1,0:T(8,128)} %fusion.23), kind=kOutput, calls=%fused_computation.8 | convolution fusion | flops 65875869696 | bytes 89915392 | tf_op jit(solution)/gta,gtb->gab/dot_general | solution.py:19
  548.6 31.8 %copy = bf16[7168,1792]{1,0:T(8,128)(2,1)} copy(bf16[7168,1792]{0,1:T(8,128)(2,1)} %fusion.1) | data formatting | bytes 51380224
  580.4 107.6 %convolution_convert_fusion = bf16[1792,7168]{1,0:T(8,128)(2,1)} fusion(bf16[2560,7168]{1,0:T(8,128)(2,1)} %all-gather.10.cloned.1.call-done, bf16[2560,1792]{1,0:T(8,128)(2,1)} %param.2), kind=kOutput, calls=%fused_computation.5 | convolution fusion | flops 65825406976 | bytes 71565312 | tf_op jit(solution)/gta,gtb->gab/dot_general | solution.py:19
  688.0 0.0 reduce-scatter.4.cloned.1.call-done
Async XLA Ops:
  7.2 214.4 %all-gather.10.cloned.1.call-start = ((), (), s32[]{:S(2)}) async-start(), calls=%async_computation.1 | async-start | bytes 38993920 | tf_op args[1]
  8.0 423.2 %all-gather.12.cloned.1.call-start = ((), (), s32[]{:S(2)}) async-start(), calls=%async_computation.2 | async-start | bytes 38993920 | tf_op jit(solution)/reshape | solution.py:18
  8.8 679.2 %reduce-scatter.4.cloned.1.call-start = ((), (), s32[]{:S(2)}) async-start(), calls=%async_computation.3 | async-start | bytes 38993920
Sparse Core Ops, SparseCore 0:
  10.0 211.5 all-gather.9
  223.6 207.5 all-gather.11
  435.2 204.8 reduce-scatter.3
where the time goes:
time: 695 us
  matrix products  407 us (59%)
  waiting for transfers between devices  241 us (35%)
  local copies, waits for them, and re-layouts  31.8 us (5%)
  between operations  13.8 us (2%)
    dot_general x2, matrix products, by_group(): jnp.einsum('gta,gtb->gab', a, b, preferred_element_type=jnp.float32)  225 us
    unnamed x5, waiting for transfers between devices  214 us
    dot_general x1, matrix products, step(): dx = jnp.dot(d_pre, w_in.T)  106 us
    dot_general x1, matrix products, step(): d_hidden = jnp.dot(dy, w_down.T, preferred_element_type=jnp.float32)  76.2 us
    unnamed x1, local copies, waits for them, and re-layouts  31.8 us
    reshape x1, waiting for transfers between devices, by_group(): a, b = (t.reshape(groups, -1, t.shape[-1]) for t in (a, b))  27.2 us
  transfers between devices with their start and end apart: 3, of which 2 were waited for; matrix products, arithmetic and copies ran while one was open for 63% of the time, Pallas kernels for 0%

commit v1 on v0

v1 whole, which is shorter than its diff:
```python
import jax
import jax.numpy as jnp
from jax import lax
from jax.experimental import pallas as pl
from jax.experimental.pallas import tpu as pltpu
from jax.sharding import PartitionSpec as P


def act(pre):
    return jax.nn.gelu(pre)


def tn_kernel(a_ref, b_ref, o_ref):
    o_ref[...] = lax.dot_general(
        a_ref[...], b_ref[...], (((0,), (0,)), ((), ())), preferred_element_type=jnp.float32
    ).astype(o_ref.dtype)


def tn_matmul(a, b, tile):
    rows, columns = a.shape
    width = b.shape[1]
    return pl.pallas_call(
        tn_kernel,
        grid=(columns // tile,),
        in_specs=[
            pl.BlockSpec((rows, tile), lambda i: (0, i)),
            pl.BlockSpec((rows, width), lambda i: (0, 0)),
        ],
        out_specs=pl.BlockSpec((tile, width), lambda i: (i, 0)),
        out_shape=jax.ShapeDtypeStruct((columns, width), a.dtype),
        compiler_params=pltpu.CompilerParams(vmem_limit_bytes=60 * 1024 * 1024),
        cost_estimate=pl.CostEstimate(
            flops=2 * rows * columns * width,
            bytes_accessed=2 * (rows * columns + rows * width + columns * width),
            transcendentals=0,
        ),
        name="tn_matmul",
    )(a, b)


def solution(mesh):
    def step(x, dy, pre, w_in, w_down):
        dy_all = lax.all_gather(dy, "tp", tiled=True)
        x, dy_all = lax.optimization_barrier((x, dy_all))
        x_all = lax.all_gather(x, "tp", tiled=True)
        hidden, back = jax.vjp(act, pre.astype(jnp.float32))
        d_hidden = jnp.dot(dy_all, w_down.T, preferred_element_type=jnp.float32)
        d_pre = back(d_hidden)[0].astype(jnp.bfloat16)
        dx = jnp.dot(d_pre, w_in.T, preferred_element_type=jnp.float32).astype(jnp.bfloat16)
        dx = lax.psum_scatter(dx, "tp", tiled=True)
        dw_down = jnp.dot(hidden.astype(jnp.bfloat16).T, dy_all, preferred_element_type=jnp.float32)
        return dx, tn_matmul(x_all, d_pre, 512), dw_down.astype(jnp.bfloat16)

    tokens = P(("dp", "tp"), None)
    return jax.shard_map(
        step,
        mesh=mesh,
        in_specs=(tokens, tokens, P("dp", "tp"), P(None, "tp"), P("tp", None)),
        out_specs=(tokens, P("dp", "tp"), tokens),
        check_vma=False,
    )
```

time: 695 us -> 647 us (0.931)
  matrix products: 407 us -> 272 us
  Pallas kernels: 0 us -> 75.1 us
  waiting for transfers between devices: 241 us -> 286 us
  local copies, waits for them, and re-layouts: 31.8 us -> 0 us
    all_gather x0 -> x2, waiting for transfers between devices: none -> 214 us  [the longest x1 214 us: step(): dy_all = lax.all_gather(dy, 'tp', tiled=True)]
    unnamed x5 -> x3, waiting for transfers between devices: 214 us -> 0.83 us
    dot_general x4 -> x3, matrix products: 407 us -> 272 us  [the longest x1 108 us: step(): jnp.dot(hidden.astype(jnp.bfloat16).T, dy_all, preferred_element_type=jnp...]
    pallas_call x0 -> x1, Pallas kernels: none -> 75.1 us  [tn_matmul(): pl.pallas_call(tn_kernel, grid=(columns // tile,), in_specs=[pl.BlockSpec...]
    reduce_scatter x0 -> x1, waiting for transfers between devices: none -> 71.2 us  [step(): dx = lax.psum_scatter(dx, 'tp', tiled=True)]
    unnamed x1 -> x0, local copies, waits for them, and re-layouts: 31.8 us -> none
    reshape x1 -> x0, waiting for transfers between devices: 27.2 us -> none  [by_group(): a, b = (t.reshape(groups, -1, t.shape[-1]) for t in (a, b))]
  transfers between devices with their start and end apart: 3 -> 3, of which waited for: 2 -> 2; matrix products, arithmetic and copies ran while one was open for 63% -> 42% of each run, Pallas kernels for 0% -> 12%
where the time goes in v1:
time: 647 us
  waiting for transfers between devices  286 us (44%)
  matrix products  272 us (42%)
  Pallas kernels  75.1 us (12%)
  between operations  13.8 us (2%)
    all_gather x1, waiting for transfers between devices, step(): dy_all = lax.all_gather(dy, 'tp', tiled=True)  214 us
    dot_general x1, matrix products, step(): jnp.dot(hidden.astype(jnp.bfloat16).T, dy_all, preferred_element_type=jnp...  108 us
    dot_general x1, matrix products, step(): d_hidden = jnp.dot(dy_all, w_down.T, preferred_element_type=jnp.float32)  88.7 us
    dot_general x1, matrix products, step(): jnp.dot(d_pre, w_in.T, preferred_element_type=jnp.float32)  75.5 us
    pallas_call x1, Pallas kernels, tn_matmul(): pl.pallas_call(tn_kernel, grid=(columns // tile,), in_specs=[pl.BlockSpec...  75.1 us
    reduce_scatter x1, waiting for transfers between devices, step(): dx = lax.psum_scatter(dx, 'tp', tiled=True)  71.2 us
  transfers between devices with their start and end apart: 3, of which 2 were waited for; matrix products, arithmetic and copies ran while one was open for 42% of the time, Pallas kernels for 12%

profile of v1, /device:TPU:97, one launch (start us, length us, event | category | flops | bytes accessed | tf_op | source)
XLA Modules:
  0.0 646.7 jit_solution(3876803670116411117)
XLA Ops:
  7.2 0.1 all-gather.3.cloned.1.call-start
  7.2 0.7 all-gather.3.cloned.1.call-update
  8.0 0.1 all-gather.5.cloned.1.call-start
  8.0 213.6 %all-gather.3.cloned.1.call-done = bf16[2560,7168]{1,0:T(8,128)(2,1)} async-done(((bf16[160,7168]{1,0:T(8,128)(2,1)}), bf16[2560,7168]{1,0:T(8,128)(2,1)}) %all-gather.3.cloned.1.call-update) | async-done | bytes 36700176 | tf_op jit(solution)/shard_map/all_gather | solution.py:43
  221.6 0.1 all-gather.5.cloned.1.call-update
  221.7 0.1 reduce-scatter.2.cloned.1.call-start
  221.7 88.7 %fusion.3.b_ref = bf16[2560,1792]{1,0:T(8,128)(2,1)} fusion(bf16[2560,1792]{1,0:T(8,128)(2,1)} %param.7, bf16[2560,7168]{1,0:T(8,128)(2,1)} %all-gather.3.cloned.1.call-done, bf16[1792,7168]{1,0:T(8,128)(2,1)} %param.9), kind=kOutput, calls=%fused_computation.10 | convolution fusion | flops 65863024640 | bytes 80740352 | tf_op jit(solution)/shard_map/dot_general | solution.py:47
  310.4 75.5 %convolution_convert_fusion = bf16[2560,7168]{1,0:T(8,128)(2,1)} fusion(bf16[2560,1792]{1,0:T(8,128)(2,1)} %fusion.3.b_ref, bf16[7168,1792]{1,0:T(8,128)(2,1)} %param.8), kind=kOutput, calls=%fused_computation | convolution fusion | flops 65785036800 | bytes 71565312 | tf_op jit(solution)/shard_map/dot_general | solution.py:49
  386.0 0.1 reduce-scatter.2.cloned.1.call-update
  386.0 107.8 %convolution_convert_fusion.1 = bf16[1792,7168]{1,0:T(8,128)(2,1)} fusion(bf16[2560,7168]{1,0:T(8,128)(2,1)} %all-gather.3.cloned.1.call-done, bf16[2560,1792]{1,0:T(8,128)(2,1)} %param.7), kind=kOutput, calls=%fused_computation.6 | convolution fusion | flops 65825406976 | bytes 71565312 | tf_op jit(solution)/shard_map/dot_general | solution.py:51
  493.8 0.0 all-gather.5.cloned.1.call-done.a_ref
  493.8 75.1 %tn_matmul.1 = bf16[7168,1792]{1,0:T(8,128)(2,1)} custom-call(bf16[2560,7168]{1,0:T(8,128)(2,1)} %all-gather.5.cloned.1.call-done.a_ref, bf16[2560,1792]{1,0:T(8,128)(2,1)} %fusion.3.b_ref), custom_call_target="tpu_custom_call" | custom-call | flops 65766686720 | bytes 71565312 | tf_op jit(solution)/shard_map/tn_matmul/pallas_call | solution.py:22
  568.9 71.2 %reduce-scatter.2.cloned.1.call-done = bf16[160,7168]{1,0:T(8,128)(2,1)} async-done(((bf16[2560,7168]{1,0:T(8,128)(2,1)}), bf16[160,7168]{1,0:T(8,128)(2,1)}) %reduce-scatter.2.cloned.1.call-update) | async-done | bytes 2293776 | tf_op jit(solution)/shard_map/reduce_scatter | solution.py:50
Async XLA Ops:
  7.2 214.4 %all-gather.3.cloned.1.call-start = ((), (), s32[]{:S(2)}) async-start(), calls=%async_computation.1 | async-start | bytes 38993920 | tf_op jit(solution)/shard_map/all_gather | solution.py:43
  8.0 485.9 %all-gather.5.cloned.1.call-start = ((), (), s32[]{:S(2)}) async-start(), calls=%async_computation.3 | async-start | bytes 38993920 | tf_op jit(solution)/shard_map/all_gather | solution.py:45
  221.7 418.4 %reduce-scatter.2.cloned.1.call-start = ((), (), s32[]{:S(2)}) async-start(), calls=%async_computation.2 | async-start | bytes 38993920 | tf_op jit(solution)/shard_map/reduce_scatter | solution.py:50
Sparse Core Ops, SparseCore 0:
  10.0 211.5 all-gather.2
  223.6 207.5 all-gather.4
  435.2 204.8 reduce-scatter.1

commit v2 on v1

v2 whole, which is shorter than its diff:
```python
import functools
import math

import jax
import jax.numpy as jnp
from jax import lax
from jax.experimental import pallas as pl
from jax.experimental.pallas import tpu as pltpu
from jax.sharding import PartitionSpec as P

MESH = pl.DeviceIdType.MESH
TILE = 256


def act(pre):
    return jax.nn.gelu(pre)


def tn_kernel(a_ref, b_ref, o_ref):
    o_ref[...] = lax.dot_general(
        a_ref[...], b_ref[...], (((0,), (0,)), ((), ())), preferred_element_type=jnp.float32
    ).astype(o_ref.dtype)


def tn_matmul(a, b, tile, tile_b=False):
    rows, height = a.shape
    width = b.shape[1]
    whole, cut = lambda i: (0, 0), lambda i: (0, i)
    return pl.pallas_call(
        tn_kernel,
        grid=((width if tile_b else height) // tile,),
        in_specs=[
            pl.BlockSpec((rows, height if tile_b else tile), whole if tile_b else cut),
            pl.BlockSpec((rows, tile if tile_b else width), cut if tile_b else whole),
        ],
        out_specs=pl.BlockSpec((height, tile) if tile_b else (tile, width), cut if tile_b else lambda i: (i, 0)),
        out_shape=jax.ShapeDtypeStruct((height, width), a.dtype),
        compiler_params=pltpu.CompilerParams(vmem_limit_bytes=60 * 1024 * 1024),
        cost_estimate=pl.CostEstimate(
            flops=2 * rows * height * width,
            bytes_accessed=2 * (rows * height + rows * width + height * width),
            transcendentals=0,
        ),
        name="tn_matmul",
    )(a, b)


STEPS = ((1, 0), (-1, 0), (0, 1), (0, -1))


def pieces_of(link):
    along_x, up = link < 2, link % 2 == 0
    mine = (0, 1) if along_x else (2, 3)
    other = (2, 3) if along_x else (0, 1)
    if not up:
        mine, other = mine[::-1], other[::-1]
    back = -1 if up else 1

    def at(first, second):
        return (first, second) if along_x else (second, first)

    return (
        [(*at(0, 0), q) for q in mine + other],
        [(*at(back, 0), mine[0])],
        [(*at(0, s), q) for s, order in ((-1, (0, 1)), (1, (1, 0))) for q in (min(other) + order[0], min(other) + order[1])],
        [(*at(0, 2), q) for q in other],
        [(*at(back, s), other[0]) for s in (0, -1, 1, 2)],
    )


class Gather:
    def __init__(self, own, every, send_sem, recv_sem, me, side):
        self.own, self.every, self.send_sem, self.recv_sem = own, every, send_sem, recv_sem
        self.me, self.side, self.rows = me, side, own.shape[0]
        self.unit = self.rows // 4
        self.sent, self.pending = [], {}
        for link, (dx, dy) in enumerate(STEPS):
            flat = [p for stage in pieces_of(link) for p in stage]
            for k, (ox, oy, q) in enumerate(flat):
                key = self.key(ox - dx, oy - dy, q)
                assert key not in self.pending
                self.pending[key] = (link, k)
        self.arrival = dict(self.pending)

    def key(self, ox, oy, q):
        return ox % self.side, oy % self.side, q

    def start_row(self, ox, oy):
        x, y = (lax.rem(m + (o % self.side), self.side) for m, o in zip(self.me, (ox, oy)))
        return pl.multiple_of((x * self.side + y) * self.rows, self.unit)

    def place(self, ox, oy, q):
        return self.every.at[pl.ds(pl.multiple_of(self.start_row(ox, oy) + q * self.unit, 8), self.unit)]

    def copy(self, link, k, source, target):
        dx, dy = STEPS[link]
        x, y = (lax.rem(m + d + self.side, self.side) for m, d in zip(self.me, (dx, dy)))
        return pltpu.make_async_remote_copy(
            src_ref=source,
            dst_ref=target,
            send_sem=self.send_sem.at[link, k],
            recv_sem=self.recv_sem.at[link, k],
            device_id={"tp": x * self.side + y},
            device_id_type=MESH,
        )

    def wait(self, ox, oy, q):
        found = self.pending.pop(self.key(ox, oy, q), None)
        if found is not None:
            place = self.place(ox, oy, q)
            self.copy(*found, place, place).wait_recv()

    def send(self, stage, only=slice(None)):
        todo = [(link, pieces_of(link)) for link in range(4)]
        count = len(todo[0][1][stage])
        for i in range(count)[only]:
            for link, stages in todo:
                k = sum(len(s) for s in stages[:stage]) + i
                ox, oy, q = stages[stage][i]
                place = self.place(ox, oy, q)
                if (ox, oy) == (0, 0):
                    source = self.own.at[pl.ds(q * self.unit, self.unit)]
                else:
                    self.wait(ox, oy, q)
                    source = place
                self.copy(link, k, source, place).start()
                self.sent.append((link, k, place))

    def wait_shard(self, ox, oy):
        for q in range(4):
            self.wait(ox, oy, q)

    def finish(self):
        for key in list(self.pending):
            self.wait(*key)
        for link, k, place in self.sent:
            self.copy(link, k, place, place).wait_send()


def gather_kernel(
    side, x_ref, dy_ref, pre_ref, w_down_ref, w_in_ref,
    x_all, dy_all, hidden_ref, d_pre_ref, dx_ref,
    w_down, w_in, dy_buf, pre_buf, hidden_buf, d_pre_buf, dx_buf,
    x_send, x_recv, dy_send, dy_recv, load_sem, store_sem, weight_sem,
):
    rows, depth = dy_ref.shape
    width = pre_ref.shape[1]
    t = lax.axis_index("tp")
    me = lax.div(t, side), lax.rem(t, side)

    barrier = pltpu.get_barrier_semaphore()
    for dx, dy in STEPS:
        x, y = (lax.rem(m + d + side, side) for m, d in zip(me, (dx, dy)))
        pl.semaphore_signal(barrier, inc=1, device_id={"tp": x * side + y}, device_id_type=MESH)
    pl.semaphore_wait(barrier, 4)

    dys = Gather(dy_ref, dy_all, dy_send, dy_recv, me, side)
    xs = Gather(x_ref, x_all, x_send, x_recv, me, side)
    dys.send(0)
    loads = [
        pltpu.make_async_copy(w_down_ref, w_down, weight_sem.at[0]),
        pltpu.make_async_copy(w_in_ref, w_in, weight_sem.at[1]),
    ]
    for load in loads:
        load.start()

    def compute(ox, oy, own=None):
        x, y = lax.rem(me[0] + ox + side, side), lax.rem(me[1] + oy + side, side)
        here = pl.ds(pl.multiple_of((x * side + y) * rows, rows), rows)
        copies = [
            pltpu.make_async_copy(dy_all.at[here] if own is None else own, dy_buf, load_sem.at[0]),
            pltpu.make_async_copy(pre_ref.at[here], pre_buf, load_sem.at[1]),
        ]
        for c in copies:
            c.start()
        for c in copies:
            c.wait()

        @pl.loop(0, width // TILE)
        def _(n):
            tile = pl.ds(pl.multiple_of(n * TILE, TILE), TILE)
            d_hidden = lax.dot_general(
                dy_buf[...], w_down[tile, :], (((1,), (1,)), ((), ())), preferred_element_type=jnp.float32
            )
            hidden, back = jax.vjp(act, pre_buf[:, tile].astype(jnp.float32))
            hidden_buf[:, tile] = hidden.astype(hidden_buf.dtype)
            d_pre_buf[:, tile] = back(d_hidden)[0].astype(d_pre_buf.dtype)

        @pl.loop(0, depth // TILE)
        def _(n):
            tile = pl.ds(pl.multiple_of(n * TILE, TILE), TILE)
            dx_buf[:, tile] = lax.dot_general(
                d_pre_buf[...], w_in[tile, :], (((1,), (1,)), ((), ())), preferred_element_type=jnp.float32
            ).astype(dx_buf.dtype)

        copies = [
            pltpu.make_async_copy(hidden_buf, hidden_ref.at[here], store_sem.at[0]),
            pltpu.make_async_copy(d_pre_buf, d_pre_ref.at[here], store_sem.at[1]),
            pltpu.make_async_copy(dx_buf, dx_ref.at[here], store_sem.at[2]),
        ]
        if own is not None:
            copies.append(pltpu.make_async_copy(dy_buf, dy_all.at[here], store_sem.at[3]))
        for c in copies:
            c.start()
        for c in copies:
            c.wait()

    def compute_many(offsets, count):
        pl.loop(0, count)(lambda k: compute(*offsets(k)))

    for load in loads:
        load.wait()
    dys.send(1)
    compute(0, 0, dy_ref)
    dys.send(2)
    for ox, oy in STEPS:
        dys.wait_shard(ox, oy)
    compute_many(lambda k: ((1 - 2 * k), 0), 2)
    dys.send(3)
    compute_many(lambda k: (0, (1 - 2 * k)), 2)
    dys.send(4)
    xs.send(0)
    for ox, oy in ((1, 1), (1, -1), (-1, 1), (-1, -1)):
        dys.wait_shard(ox, oy)
    compute_many(lambda k: (1 - 2 * lax.rem(k, 2), 1 - 2 * lax.div(k, 2)), 4)
    for ox, oy in ((2, 0), (0, 2)):
        dys.wait_shard(ox, oy)
    compute_many(lambda k: (2 * k, 2 - 2 * k), 2)
    xs.send(1)
    xs.send(2)
    for ox, oy in ((2, 1), (2, -1), (1, 2), (-1, 2), (2, 2)):
        dys.wait_shard(ox, oy)
    compute_many(lambda k: (2, 1 - 2 * k), 2)
    compute_many(lambda k: (1 - 2 * k, 2), 2)
    xs.send(3)
    compute(2, 2)
    own = pltpu.make_async_copy(x_ref, dy_buf, load_sem.at[0])
    own.start()
    own.wait()
    own = pltpu.make_async_copy(dy_buf, x_all.at[pl.ds(pl.multiple_of(t * rows, rows), rows)], store_sem.at[3])
    own.start()
    own.wait()
    xs.send(4)
    dys.finish()
    xs.finish()


def gather_and_differentiate(x, dy, pre, w_down, w_in, group):
    side = math.isqrt(group)
    assert side == 4 and side * side == group
    rows, depth = dy.shape
    width = pre.shape[1]
    assert rows % 32 == 0 and width % TILE == 0 and depth % TILE == 0
    like = jax.ShapeDtypeStruct
    any_space = pl.BlockSpec(memory_space=pl.ANY)
    flops = 4 * group * rows * depth * width
    return pl.pallas_call(
        functools.partial(gather_kernel, side),
        out_shape=(
            like((group * rows, depth), x.dtype),
            like((group * rows, depth), x.dtype),
            like((group * rows, width), x.dtype),
            like((group * rows, width), x.dtype),
            like((group * rows, depth), x.dtype),
        ),
        in_specs=[any_space] * 5,
        out_specs=[any_space] * 5,
        scratch_shapes=[
            pltpu.VMEM((width, depth), x.dtype),
            pltpu.VMEM((depth, width), x.dtype),
            pltpu.VMEM((rows, depth), x.dtype),
            pltpu.VMEM((rows, width), x.dtype),
            pltpu.VMEM((rows, width), x.dtype),
            pltpu.VMEM((rows, width), x.dtype),
            pltpu.VMEM((rows, depth), x.dtype),
            pltpu.SemaphoreType.DMA((4, 15)),
            pltpu.SemaphoreType.DMA((4, 15)),
            pltpu.SemaphoreType.DMA((4, 15)),
            pltpu.SemaphoreType.DMA((4, 15)),
            pltpu.SemaphoreType.DMA((2,)),
            pltpu.SemaphoreType.DMA((4,)),
            pltpu.SemaphoreType.DMA((2,)),
        ],
        compiler_params=pltpu.CompilerParams(
            collective_id=0, has_side_effects=True, vmem_limit_bytes=67_043_328
        ),
        cost_estimate=pl.CostEstimate(flops=flops, bytes_accessed=2 * group * rows * (5 * depth + 3 * width), transcendentals=0),
        name="gather_and_differentiate",
    )(x, dy, pre, w_down, w_in)


def solution(mesh):
    group = mesh.shape["tp"]

    def step(x, dy, pre, w_in, w_down):
        x_all, dy_all, hidden, d_pre, dx = gather_and_differentiate(x, dy, pre, w_down, w_in, group)
        dx = lax.psum_scatter(dx, "tp", tiled=True)
        dw_down = tn_matmul(hidden, dy_all, 512, tile_b=True)
        return dx, tn_matmul(x_all, d_pre, 512), dw_down

    tokens = P(("dp", "tp"), None)
    return jax.shard_map(
        step,
        mesh=mesh,
        in_specs=(tokens, tokens, P("dp", "tp"), P(None, "tp"), P("tp", None)),
        out_specs=(tokens, P("dp", "tp"), tokens),
        check_vma=False,
    )
```

time: 647 us -> 723 us (1.12)
  Pallas kernels: 75.1 us -> 652 us
  matrix products: 272 us -> 0 us
  waiting for transfers between devices: 286 us -> 56.4 us
    pallas_call x1 -> x3, Pallas kernels: 75.1 us -> 652 us  [the longest x1 501 us: gather_and_differentiate(): pl.pallas_call(functools.partial(gather_kernel, side), out_shape=(like((g...]
    dot_general x3 -> x0, matrix products: 272 us -> none  [the longest x1 108 us: step(): jnp.dot(hidden.astype(jnp.bfloat16).T, dy_all, preferred_element_type=jnp...]
    all_gather x2 -> x0, waiting for transfers between devices: 214 us -> none  [the longest x1 214 us: step(): dy_all = lax.all_gather(dy, 'tp', tiled=True)]
    reduce_scatter x1, waiting for transfers between devices: 71.2 us -> 56.3 us  [step(): dx = lax.psum_scatter(dx, 'tp', tiled=True)]
  transfers between devices with their start and end apart: 3 -> 1, of which waited for: 2 -> 1; matrix products, arithmetic and copies ran while one was open for 42% -> 0% of each run, Pallas kernels for 12% -> 21%
where the time goes in v2:
time: 723 us; the launch traced here: 722 us
  Pallas kernels  652 us (90%)
  waiting for transfers between devices  56.4 us (8%)
  between operations  14.1 us (2%)
    pallas_call x1, Pallas kernels, gather_and_differentiate(): pl.pallas_call(functools.partial(gather_kernel, side), out_shape=(like((g...  501 us
    pallas_call x2, Pallas kernels, tn_matmul(): pl.pallas_call(tn_kernel, grid=((width if tile_b else height) // tile,),...  151 us
    reduce_scatter x1, waiting for transfers between devices, step(): dx = lax.psum_scatter(dx, 'tp', tiled=True)  56.3 us
  transfers between devices with their start and end apart: 1, of which 1 were waited for; matrix products, arithmetic and copies ran while one was open for 0% of the time, Pallas kernels for 21%

profile of v2, /device:TPU:97, one launch (start us, length us, event | category | flops | bytes accessed | tf_op | source)
XLA Modules:
  0.0 722.3 jit_solution(9154907035745191213)
XLA Ops:
  7.2 0.1 reduce-scatter.2.cloned.1.call-start
  7.2 501.0 %gather_and_differentiate.1 = (bf16[2560,7168]{1,0:T(8,128)(2,1)}, bf16[2560,7168]{1,0:T(8,128)(2,1)}, bf16[2560,1792]{1,0:T(8,128)(2,1)}, bf16[2560,1792]{1,0:T(8,128)(2,1)}, bf16[2560,7168]{1,0:T(8,128)(2,1)}) custom-call(bf16[160,7168]{1,0:T(8,128)(2,1)} %x_ref.1, bf16[160,7168]{1,0:T(8,128)(2,1)} %dy_ref.1, bf16[2560,1792]{1,0:T(8,128)(2,1)} %pre_ref.1, ...), custom_call_target="tpu_custom_call" | custom-call | flops 131533373440 | bytes 211025920 | tf_op jit(solution)/shard_map/gather_and_differentiate/pallas_call | solution.py:257
  508.2 0.1 reduce-scatter.2.cloned.1.call-update
  508.3 75.3 %tn_matmul.2 = bf16[7168,1792]{1,0:T(8,128)(2,1)} custom-call(bf16[2560,7168]{1,0:T(8,128)(2,1)} %get-tuple-element.9.a_ref, bf16[2560,1792]{1,0:T(8,128)(2,1)} %get-tuple-element.10.b_ref), custom_call_target="tpu_custom_call" | custom-call | flops 65766686720 | bytes 71565312 | tf_op jit(solution)/shard_map/tn_matmul/pallas_call | solution.py:29
  583.6 75.5 %tn_matmul.3 = bf16[1792,7168]{1,0:T(8,128)(2,1)} custom-call(bf16[2560,1792]{1,0:T(8,128)(2,1)} %get-tuple-element.11.a_ref, bf16[2560,7168]{1,0:T(8,128)(2,1)} %get-tuple-element.12.b_ref), custom_call_target="tpu_custom_call" | custom-call | flops 65766686720 | bytes 71565312 | tf_op jit(solution)/shard_map/tn_matmul/pallas_call | solution.py:29
  659.1 56.3 %reduce-scatter.2.cloned.1.call-done = bf16[160,7168]{1,0:T(8,128)(2,1)} async-done(((bf16[2560,7168]{1,0:T(8,128)(2,1)}), bf16[160,7168]{1,0:T(8,128)(2,1)}) %reduce-scatter.2.cloned.1.call-update) | async-done | bytes 2293776 | tf_op jit(solution)/shard_map/reduce_scatter | solution.py:297
Async XLA Ops:
  7.2 708.3 %reduce-scatter.2.cloned.1.call-start = ((), (), s32[]{:S(2)}) async-start(), calls=%async_computation.1 | async-start | bytes 38993920 | tf_op jit(solution)/shard_map/reduce_scatter | solution.py:297
Sparse Core Ops, SparseCore 0:
  508.4 207.0 reduce-scatter.1
